TPU v7x, 8 devices: a whole 2x2x1 slice. The times are simulated.
8 devices in a mesh: dp: 1 (over z), ep: 8 (over y, x, core).
Axes of the slice: x: 2, y: 2, z: 1, core: 2. Of those that a mesh axis runs over, the one named last changes fastest.
Arguments:
- hidden: bfloat16 [2048, 1024], P(('dp', 'ep'))
- k_cache: bfloat16 [2048, 128, 8, 64], P(('dp', 'ep'))
- v_cache: bfloat16 [2048, 128, 8, 64], P(('dp', 'ep'))
- seq_lens: int32 [2048], P(('dp', 'ep'))
- expert_ids: int32 [2048, 8], P(('dp', 'ep'))
- ln_attn: bfloat16 [1024], replicated
- w_q: bfloat16 [1024, 1024], replicated
- w_k: bfloat16 [1024, 512], replicated
- w_v: bfloat16 [1024, 512], replicated
- q_gain: bfloat16 [64], replicated
- k_gain: bfloat16 [64], replicated
- w_o: bfloat16 [1024, 1024], replicated
- ln_moe: bfloat16 [1024], replicated
- w_router: bfloat16 [1024, 32], replicated
- w_gate: bfloat16 [32, 1024, 512], P('ep')
- w_up: bfloat16 [32, 1024, 512], P('ep')
- w_down: bfloat16 [32, 512, 1024], P('ep')
Outputs:
- output 1: bfloat16 [2048, 1024], P(('dp', 'ep'))
- output 2: bfloat16 [2048, 128, 8, 64], P(('dp', 'ep'))
- output 3: bfloat16 [2048, 128, 8, 64], P(('dp', 'ep'))
All inputs are finite; a program needn't handle non-finite values.
Results may differ from a plain program's by a relative error of at most 0.0112857.
Values are sent between devices in bfloat16 or wider.
A program may use at most 1 GiB of HBM per device.

v0:
```python
import functools
import numpy as np
import jax, jax.numpy as jnp
from jax import lax
from jax.experimental import pallas as pl
from jax.experimental.pallas import tpu as pltpu
from jax.sharding import PartitionSpec as P
EPS=1e-6; ROPE_BASE=1e6
F32=jnp.float32; BF=jnp.bfloat16

def attn_body(cfg, lens_hbm, ids_hbm, lnm_hbm, h_hbm, wo_hbm, wr_hbm, k_hbm, v_hbm, *refs):
    sb, nb, lag, lo, n, first, last = cfg
    n_kv, hd, dk = 8, 64, 512
    if first:
        lna_hbm, qg_hbm, kg_hbm, freq_hbm, wq_hbm, wk_hbm, wv_hbm = refs[:7]
        refs = refs[7:]
    else:
        qe_ref, qo_ref, kt_ref, vt_ref, _, _, gp_ref = refs[:7]
        refs = refs[7:]
    ko_hbm, vo_hbm, y_ref, r_ref, gt_ref = refs[:5]
    refs = refs[5:]
    if first and not last:
        qeb_ref, qob_ref, ktb_ref, vtb_ref = refs[:4]
        refs = refs[4:]
    kb, vb, woe, woo, h_ref, ae_ref, ao_ref, lens_s, ids_ref, lnm_ref, wr_ref, isem, osem, wsem = refs[:14]
    if first:
        qe_ref, qo_ref, kt_ref, vt_ref, wq, wk, wv, lens_ref, lna_ref, qg_ref, kg_ref, freq_ref, qsem = refs[14:]
    steps = n // sb
    per = 128 // sb
    def cin(g, which):
        s = lax.rem(g, nb)
        r, b = ((k_hbm, kb), (v_hbm, vb))[which]
        return pltpu.make_async_copy(r.at[pl.ds(lo + g*sb, sb)], b.at[s], isem.at[which, s])
    def cout(g, which):
        s = lax.rem(g, nb)
        r, b = ((ko_hbm, kb), (vo_hbm, vb))[which]
        return pltpu.make_async_copy(b.at[s], r.at[pl.ds(lo + g*sb, sb)], osem.at[which, s])
    late = [pltpu.make_async_copy(a, b, wsem.at[i]) for i, (a, b) in enumerate(((wo_hbm.at[:, 0], woe), (wo_hbm.at[:, 1], woo), (ids_hbm, ids_ref), (lnm_hbm, lnm_ref), (wr_hbm, wr_ref)))]
    early = [pltpu.make_async_copy(h_hbm if first else h_hbm.at[pl.ds(lo, n)], h_ref, wsem.at[5]), pltpu.make_async_copy(lens_hbm, lens_s, wsem.at[6])]
    if first:
        early += [pltpu.make_async_copy(a, b, qsem.at[i]) for i, (a, b) in enumerate(((lens_hbm, lens_ref), (lna_hbm, lna_ref), (qg_hbm, qg_ref), (kg_hbm, kg_ref), (freq_hbm, freq_ref), (wq_hbm, wq), (wk_hbm, wk), (wv_hbm, wv)))]
    for c in early:
        c.start()
    if first:
        cin(0, 0).start(); cin(0, 1).start()
        for c in early:
            c.wait()
    for g in range(*((1, nb) if first else (0, 2))):
        cin(g, 0).start(); cin(g, 1).start()
    for c in late:
        c.start()
    if first:
        na = h_ref.shape[0]
        h = h_ref[...].astype(F32)
        x = (h * lax.rsqrt(jnp.mean(h*h, axis=-1, keepdims=True) + EPS) * lna_ref[...].astype(F32)[None, :]).astype(BF)
        ang = freq_ref[...] * lens_ref[...].astype(F32)[None, :]
        cos_v = jnp.cos(ang)[None]; sin_v = jnp.sin(ang)[None]
        half = hd // 2
        eye = lax.broadcasted_iota(jnp.int32, (hd, hd), 0) == lax.broadcasted_iota(jnp.int32, (hd, hd), 1)
        def norm_rope(w_ref, g_ref):
            gain = jnp.sum(jnp.where(eye, g_ref[...].astype(F32)[None, :], 0.0), axis=1, keepdims=True)
            p = jnp.dot(x, w_ref[...], preferred_element_type=F32)
            p = p.T.reshape(-1, hd, na)
            p = p * lax.rsqrt(jnp.mean(p*p, axis=1, keepdims=True) + EPS) * gain[None]
            lo_, hi = p[:, :half], p[:, half:]
            return jnp.concatenate([lo_*cos_v - hi*sin_v, hi*cos_v + lo_*sin_v], axis=1)
        q = norm_rope(wq, qg_ref)
        q = q.reshape(n_kv, 2, hd, na)
        qe = q[:, 0].reshape(dk, na).T
        qo = q[:, 1].reshape(dk, na).T
        qe_ref[...] = qe[:n]
        qo_ref[...] = qo[:n]
        k = norm_rope(wk, kg_ref).reshape(dk, na).astype(BF).astype(F32)
        v = jnp.dot(x, wv[...], preferred_element_type=F32).T.astype(BF).astype(F32)
        for c in range(n // 128):
            kt_ref[c] = k[:, 128*c:128*c+128]
            vt_ref[c] = v[:, 128*c:128*c+128]
        if not last:
            qeb_ref[...] = qe[n:]
            qob_ref[...] = qo[n:]
            for c in range((na - n) // 128):
                ktb_ref[c] = k[:, n+128*c:n+128*c+128]
                vtb_ref[c] = v[:, n+128*c:n+128*c+128]
    else:
        for c in early:
            c.wait()

    lane = lax.broadcasted_iota(jnp.int32, (1, 128), 1)
    row = lax.broadcasted_iota(jnp.int32, (16, dk), 0)
    col = lax.broadcasted_iota(jnp.int32, (16, dk), 1) // hd
    m_even = row == col
    m_odd = row == col + n_kv

    zz = jnp.zeros((16, 128), BF)
    def fresh(t_ref, g, i):
        ln = lens_s[lo + g*sb + i]
        col = pltpu.roll(t_ref[g // per], lax.rem(ln - (lax.rem(g, per) * sb + i) + 128, 128), 1).astype(BF)
        return lane == ln, col
    def insert(buf, t_ref, g, p):
        slot = lax.rem(g, nb)
        for i in (2*p, 2*p+1):
            hit, col = fresh(t_ref, g, i)
            buf[slot, i] = jnp.where(hit, col, buf[slot, i])
    def scores(g, p, qe, qo):
        slot = lax.rem(g, nb)
        qs = [jnp.where(m_even, qe[i:i+1], jnp.where(m_odd, qo[i:i+1], 0.0)).astype(BF) for i in (2*p, 2*p+1)]
        ks = jnp.concatenate([kb[slot, 2*p], kb[slot, 2*p+1]], axis=1)
        s = jnp.dot(jnp.concatenate(qs, axis=0), ks, preferred_element_type=F32)
        return [jnp.where(lane <= lens_s[lo + g*sb + 2*p + j], s[16*j:16*j+16, 128*j:128*j+128] * (hd ** -0.5), -1e30) for j in (0, 1)]
    def combine(g, p, pr):
        slot = lax.rem(g, nb)
        p0 = pr[32*p:32*p+16]; p1 = pr[32*p+16:32*p+32]
        pp = jnp.concatenate([jnp.concatenate([p0, zz], axis=1), jnp.concatenate([zz, p1], axis=1)], axis=0)
        vv = jnp.concatenate([vb[slot, 2*p], vb[slot, 2*p+1]], axis=1)
        o = lax.dot_general(pp, vv, (((1,), (1,)), ((), ())), preferred_element_type=F32)
        ev = []; od = []
        for j in (0, 1):
            oj = o[16*j:16*j+16]
            ev.append(jnp.sum(jnp.where(m_even[:8], oj[:8], 0.0), axis=0, keepdims=True))
            od.append(jnp.sum(jnp.where(m_even[:8], oj[8:], 0.0), axis=0, keepdims=True))
        return ev, od
    def attend(g, nxt):
        rows = pl.ds(pl.multiple_of(g*sb, sb), sb)
        qe = qe_ref[rows, :]
        qo = qo_ref[rows, :]
        sc = []
        for p in range(sb // 2):
            sc += scores(g, p, qe, qo)
        s = jnp.concatenate(sc, axis=0)
        e = jnp.exp(s - jnp.max(s, axis=-1, keepdims=True))
        pr = (e / jnp.sum(e, axis=-1, keepdims=True)).astype(BF)
        oe = []; oo = []
        for p in range(sb // 2):
            ev, od = combine(g, p, pr)
            oe += ev; oo += od
            if nxt is not None:
                insert(kb, kt_ref, nxt, p)
                insert(vb, vt_ref, nxt, p)
        ae_ref[rows, :] = jnp.concatenate(oe, axis=0)
        ao_ref[rows, :] = jnp.concatenate(oo, axis=0)

    cut = n // 2
    def finish(r0, nr):
        part = slice(r0, r0 + nr)
        y = h_ref[part].astype(F32)
        y = y + (jnp.dot(ae_ref[part].astype(BF), woe[...].reshape(dk, -1), preferred_element_type=F32)
                 + jnp.dot(ao_ref[part].astype(BF), woo[...].reshape(dk, -1), preferred_element_type=F32))
        y_ref[part] = y
        r = (y * lax.rsqrt(jnp.mean(y*y, axis=-1, keepdims=True) + EPS) * lnm_ref[...].astype(F32)[None, :]).astype(BF)
        r_ref[part] = r
        lg = lax.dot_general(wr_ref[...], r, (((1,), (1,)), ((), ())), preferred_element_type=F32)
        eid = lax.broadcasted_iota(jnp.int32, lg.shape, 0)
        ids = ids_ref[:, lo+r0:lo+r0+nr]
        hot = eid == ids[0:1]
        for j in range(1, ids.shape[0]):
            hot = hot | (eid == ids[j:j+1])
        lg = jnp.where(hot, lg, -jnp.inf)
        e = jnp.where(hot, jnp.exp(lg - jnp.max(lg, axis=0, keepdims=True)), 0.0)
        gt_ref[:, lo+r0:lo+r0+nr] = e / jnp.sum(e, axis=0, keepdims=True)
    if not first:
        gt_ref[:, :lo] = gp_ref[...]

    cin(0, 0).wait(); cin(0, 1).wait()
    for p in range(sb // 2):
        insert(kb, kt_ref, jnp.int32(0), p)
        insert(vb, vt_ref, jnp.int32(0), p)
    cout(0, 0).start(); cout(0, 1).start()
    for g in range(nb if first else 2, nb):
        cin(g, 0).start(); cin(g, 1).start()

    @pl.loop(0, steps - 1)
    def _(g):
        @pl.when((g >= lag) & (g - lag + nb < steps))
        def _():
            cout(g - lag, 0).wait(); cout(g - lag, 1).wait()
            cin(g - lag + nb, 0).start(); cin(g - lag + nb, 1).start()
        @pl.when(g == cut // sb)
        def _():
            for c in late:
                c.wait()
            finish(0, cut)
        cin(g + 1, 0).wait(); cin(g + 1, 1).wait()
        attend(g, g + 1)
        cout(g + 1, 0).start(); cout(g + 1, 1).start()
    attend(jnp.int32(steps - 1), None)

    finish(cut, n - cut)
    for j in range(nb):
        cout(steps - nb + j, 0).wait(); cout(steps - nb + j, 1).wait()

def attn_call(hidden, kc, vc, seq_lens, expert_ids, ln_attn, w_q, w_k, w_v, q_gain, k_gain, w_o, ln_moe, w_router, lo, n, prev=None, cfg=(8, 8, 3)):
    ntot, d = hidden.shape
    _, dk, t = kc.shape
    hd = q_gain.shape[0]
    nk = dk // hd
    sb, nb, lag = cfg
    ne = w_router.shape[1]
    first, last = lo == 0, lo + n == ntot
    vm = pl.BlockSpec(memory_space=pltpu.VMEM)
    an = pl.BlockSpec(memory_space=pltpu.HBM)
    args = [seq_lens, expert_ids.T, ln_moe, hidden, w_o.reshape(nk, 2, hd, d), w_router.T, kc, vc]
    specs = [an]*8
    alias = {}
    shape = jax.ShapeDtypeStruct
    outs = [shape(kc.shape, BF), shape(vc.shape, BF), shape((n, d), F32), shape((n, d), BF), shape((ne, lo + n), F32)]
    ospecs = [an, an, vm, vm, vm]
    dma = pltpu.SemaphoreType.DMA
    scratch = [pltpu.VMEM((nb, sb, dk, t), BF), pltpu.VMEM((nb, sb, dk, t), BF), pltpu.VMEM((nk, hd, d), BF), pltpu.VMEM((nk, hd, d), BF),
               pltpu.VMEM((ntot if first else n, d), BF), pltpu.VMEM((n, dk), F32), pltpu.VMEM((n, dk), F32),
               pltpu.SMEM(seq_lens.shape, jnp.int32), pltpu.VMEM(expert_ids.shape[::-1], jnp.int32), pltpu.VMEM(ln_moe.shape, BF), pltpu.VMEM(w_router.shape[::-1], BF),
               dma((2, nb)), dma((2, nb)), dma((7,))]
    if first:
        freq = np.power(np.float32(ROPE_BASE), -np.arange(0, hd, 2).astype(np.float32) / np.float32(hd)).astype(np.float32).reshape(-1, 1)
        args += [ln_attn, q_gain, k_gain, jnp.asarray(freq), w_q, w_k, w_v]
        specs += [an]*7
        scratch += [pltpu.VMEM((n, dk), F32), pltpu.VMEM((n, dk), F32), pltpu.VMEM((n//128, dk, 128), F32), pltpu.VMEM((n//128, dk, 128), F32),
                    pltpu.VMEM(w_q.shape, BF), pltpu.VMEM(w_k.shape, BF), pltpu.VMEM(w_v.shape, BF),
                    pltpu.VMEM(seq_lens.shape, jnp.int32), pltpu.VMEM(ln_attn.shape, BF), pltpu.VMEM(q_gain.shape, BF), pltpu.VMEM(k_gain.shape, BF), pltpu.VMEM(freq.shape, F32), dma((8,))]
        if not last:
            m = ntot - n
            outs += [shape((m, dk), F32), shape((m, dk), F32), shape((m//128, dk, 128), F32), shape((m//128, dk, 128), F32)]
            ospecs += [vm]*4
    else:
        args += list(prev)
        specs += [vm]*4 + [an, an, vm]
        alias = {12: 0, 13: 1}
    frac = n / ntot
    return pl.pallas_call(functools.partial(attn_body, cfg + (lo, n, first, last)), out_shape=outs, in_specs=specs, out_specs=ospecs,
        input_output_aliases=alias, scratch_shapes=scratch,
        compiler_params=pltpu.CompilerParams(vmem_limit_bytes=67043328), name="attn",
        cost_estimate=pl.CostEstimate(flops=int(40*10**9*frac), bytes_accessed=int(140*10**6*frac), transcendentals=0),
    )(*args)

def cache_views(c):
    n, t, nk, hd = c.shape
    return c.transpose(0, 2, 3, 1).reshape(n, nk*hd, t), lambda z: z.reshape(n, nk, hd, t).transpose(0, 3, 1, 2)


def moe_body(r_ref, gt_ref, y_hbm, wg_own, wu_own, wd_own, wg_par, wu_par, wd_par, out_ref,
             wg, wu, wd, xr, gts, y_ref, act, acc, rbuf, wsem, ysem, agsem_s, agsem_r, gsem_s, gsem_r, rssem_s, rssem_r):
    me = lax.axis_index('ep')
    core = me % 2
    xpos = (me // 2) % 2
    ypos = me // 4
    OWN, X, Y, D = 0, 1, 2, 3
    peers = [None, ypos*4 + (1-xpos)*2 + core, (1-ypos)*4 + xpos*2 + core, (1-ypos)*4 + (1-xpos)*2 + core]
    n_loc = wg_own.shape[0]
    n_exp = 2*n_loc
    hr, hc = acc.shape[3], acc.shape[4]
    ff = wg.shape[2]

    barrier = pltpu.get_barrier_semaphore()
    for p in peers[1:]:
        pl.semaphore_signal(barrier, inc=1, device_id={"ep": p}, device_id_type=pl.DeviceIdType.MESH)

    def wcopy(e, own):
        src = (wg_own, wu_own, wd_own) if own else (wg_par, wu_par, wd_par)
        s = lax.rem(e, n_loc)
        return [pltpu.make_async_copy(a.at[s], b.at[e], wsem.at[i, e]) for i, (a, b) in enumerate(zip(src, (wg, wu, wd)))]
    for c in wcopy(jnp.int32(0), True):
        c.start()
    ahead = 2
    for e in range(1, ahead):
        for c in wcopy(jnp.int32(e), True):
            c.start()
    ycopy = pltpu.make_async_copy(y_hbm, y_ref, ysem.at[0])
    ycopy.start()
    pl.semaphore_wait(barrier, 3)

    def remote(src, dst, ss, rs, p):
        return pltpu.make_async_remote_copy(src_ref=src, dst_ref=dst, send_sem=ss, recv_sem=rs,
                                            device_id={"ep": p}, device_id_type=pl.DeviceIdType.MESH)
    ag = {}
    gc = {}
    for b in (D, X, Y):
        rows8 = pl.ds(pl.multiple_of((peers[b] // 2) * n_exp, n_exp), n_exp)
        gc[b] = remote(gt_ref.at[rows8], gts.at[b-1], gsem_s.at[b-1], gsem_r.at[b-1], peers[b])
        gc[b].start()
    for b, h in ((X, 1), (Y, 0), (X, 0), (Y, 1)):
        part = pl.ds(h*hr, hr)
        ag[b, h] = remote(r_ref.at[part], xr.at[b-1, part], agsem_s.at[b-1, h], agsem_r.at[b-1, h], peers[b])
        ag[b, h].start()
    h0, h1 = pl.ds(0, hr), pl.ds(hr, hr)
    relay = [remote(xr.at[Y-1, h0], xr.at[D-1, h0], agsem_s.at[2, 0], agsem_r.at[2, 0], peers[X]),
             remote(xr.at[X-1, h1], xr.at[D-1, h1], agsem_s.at[2, 1], agsem_r.at[2, 1], peers[Y])]

    def gates(b):
        if b == OWN:
            return gt_ref[pl.ds(pl.multiple_of((me // 2) * n_exp, n_exp), n_exp), :].T
        return gts[b-1].T

    def compute(load, g8, blocks, first=False):
        m = len(blocks) * hr
        lane8 = lax.broadcasted_iota(jnp.int32, (m, n_exp), 1)
        for b, h in blocks:
            acc[b, h] = jnp.zeros(acc.shape[2:], F32)
        def step(e, carry):
            if first:
                for c in wcopy(e, True):
                    c.wait()
                @pl.when(e + ahead < n_loc)
                def _():
                    for c in wcopy(e + ahead, True):
                        c.start()
                @pl.when((e + ahead >= n_loc) & (e + ahead < n_exp))
                def _():
                    for c in wcopy(e + ahead, False):
                        c.start()
            gcol = jnp.sum(jnp.where(lane8 == lax.rem(core * n_loc + e, n_exp), g8, 0.0), axis=1, keepdims=True)
            x = load()
            for q in range(2):
                cols = slice(q*ff//2, (q+1)*ff//2)
                g = jnp.dot(x, wg[e, :, cols], preferred_element_type=F32)
                u = jnp.dot(x, wu[e, :, cols], preferred_element_type=F32)
                act[:m, cols] = (jax.nn.silu(g) * u).astype(BF)
            a = act[:m]
            for q in range(4):
                w = hc // 2
                s = (q % 2) * w
                f = jnp.dot(a, wd[e, :, q*w:(q+1)*w], preferred_element_type=F32).astype(BF).astype(F32) * gcol
                for i, (b, h) in enumerate(blocks):
                    acc[b, h, q//2, :, s:s+w] = acc[b, h, q//2, :, s:s+w] + f[i*hr:(i+1)*hr]
            return carry
        lax.fori_loop(0, n_exp, step, 0, unroll=1 if first else 2)

    def rs(i, h, src, p):
        return remote(src, rbuf.at[i, h], rssem_s.at[i, h], rssem_r.at[i, h], p)
    sent = {}
    def send(i, h, src, b):
        sent[i, h] = rs(i, h, src, peers[b])
        sent[i, h].start()

    def rows(h):
        return slice(h*hr, (h+1)*hr)
    def diagonal(h):
        relay[h].wait_recv()
        compute(lambda: xr[D-1, rows(h)], gates(D)[rows(h)], ((D, h),))
        send(0, h, acc.at[D, h, 0], X)
        send(1, h, acc.at[D, h, 1], Y)
    def neighbours(h):
        compute(lambda: jnp.concatenate([xr[X-1, rows(1-h)], xr[Y-1, rows(h)]], axis=0),
                jnp.concatenate([gates(X)[rows(1-h)], gates(Y)[rows(h)]], axis=0), ((X, 1-h), (Y, h)))
        send(2, 1-h, acc.at[X, 1-h, 0], X)
        send(3, h, acc.at[Y, h, 1], Y)
    def own(h, first):
        compute(lambda: r_ref[rows(h)], gates(OWN)[rows(h)], ((OWN, h),), first)
    def pass_on(h):
        sent[1, h].wait_recv()
        acc[X, h, 1] = acc[X, h, 1] + rbuf[1, h]
        send(4, h, acc.at[X, h, 1], X)
        sent[0, h].wait_recv()
        acc[Y, h, 0] = acc[Y, h, 0] + rbuf[0, h]
        send(5, h, acc.at[Y, h, 0], Y)
    own(0, True)
    ag[Y, 0].wait_recv()
    relay[0].start()
    ag[X, 1].wait_recv()
    relay[1].start()
    gc[X].wait_recv(); gc[Y].wait_recv()
    neighbours(0)
    ag[X, 0].wait_recv(); ag[Y, 1].wait_recv()
    neighbours(1)
    gc[D].wait_recv()
    diagonal(0)
    diagonal(1)
    own(1, False)
    pass_on(0)
    pass_on(1)
    ycopy.wait()
    for h in (0, 1):
        sent[2, h].wait_recv()
        sent[3, h].wait_recv()
        acc[OWN, h, 0] = y_ref[rows(h), :hc] + (acc[OWN, h, 0] + rbuf[2, h])
        acc[OWN, h, 1] = y_ref[rows(h), hc:] + (acc[OWN, h, 1] + rbuf[3, h])
        sent[5, h].wait_recv()
        out_ref[rows(h), :hc] = (acc[OWN, h, 0] + rbuf[5, h]).astype(out_ref.dtype)
        sent[4, h].wait_recv()
        out_ref[rows(h), hc:] = (acc[OWN, h, 1] + rbuf[4, h]).astype(out_ref.dtype)
    for c in (*gc.values(), *ag.values(), *relay, *sent.values()):
        c.wait_send()

def moe_call(r, gt, y, w_gate, w_up, w_down, wg_p, wu_p, wd_p):
    n, d = r.shape
    nl, _, ff = w_gate.shape
    vm = pl.BlockSpec(memory_space=pltpu.VMEM)
    an = pl.BlockSpec(memory_space=pl.ANY)
    dma = pltpu.SemaphoreType.DMA
    return pl.pallas_call(moe_body,
        out_shape=jax.ShapeDtypeStruct((n, d), BF),
        in_specs=[vm, vm] + [an]*7, out_specs=vm,
        scratch_shapes=[pltpu.VMEM((2*nl, d, ff), BF), pltpu.VMEM((2*nl, d, ff), BF), pltpu.VMEM((2*nl, ff, d), BF),
            pltpu.VMEM((3, n, d), BF), pltpu.VMEM((3, 2*nl, n), F32), pltpu.VMEM((n, d), F32), pltpu.VMEM((n, ff), BF),
            pltpu.VMEM((4, 2, 2, n//2, d//2), F32), pltpu.VMEM((6, 2, n//2, d//2), F32),
            dma((3, 2*nl)), dma((1,)), dma((3, 2)), dma((3, 2)), dma((3,)), dma((3,)), dma((6, 2)), dma((6, 2))],
        compiler_params=pltpu.CompilerParams(vmem_limit_bytes=67043328, collective_id=1, has_side_effects=True), name="moe",
        cost_estimate=pl.CostEstimate(flops=26*10**9, bytes_accessed=30*10**6, transcendentals=0),
    )(r, gt, y, w_gate, w_up, w_down, wg_p, wu_p, wd_p)


def solution(mesh):
    n_group = mesh.shape['ep']
    row_spec = P(('dp', 'ep'), None)
    cache_spec = P(('dp', 'ep'), None, None, None)
    len_spec = P(('dp', 'ep'))
    rep_vec = P(None)
    rep_mat = P(None, None)
    exp_spec = P('ep', None, None)
    swap = [(i, i + 1 - 2 * (i % 2)) for i in range(n_group)]

    def local_step(hidden, k_cache, v_cache, seq_lens, expert_ids, ln_attn, w_q, w_k, w_v, q_gain, k_gain, w_o, ln_moe, w_router, w_gate, w_up, w_down):
        wg_p = lax.ppermute(w_gate, 'ep', swap)
        wu_p = lax.ppermute(w_up, 'ep', swap)
        wd_p = lax.ppermute(w_down, 'ep', swap)
        kc, back = cache_views(k_cache)
        vc, _ = cache_views(v_cache)
        ko, vo, y, r, gt = attn_call(hidden, kc, vc, seq_lens, expert_ids, ln_attn, w_q, w_k, w_v, q_gain, k_gain, w_o, ln_moe, w_router, 0, hidden.shape[0])
        out = moe_call(r, gt, y, w_gate, w_up, w_down, wg_p, wu_p, wd_p)
        return out, back(ko), back(vo)

    return jax.shard_map(local_step, mesh=mesh, in_specs=(row_spec, cache_spec, cache_spec, len_spec, row_spec, rep_vec, rep_mat, rep_mat, rep_mat, rep_vec, rep_vec, rep_mat, rep_vec, rep_mat, exp_spec, exp_spec, exp_spec), out_specs=(row_spec, cache_spec, cache_spec), check_vma=False)
```

profile of v0, /device:TPU:0, one launch (start us, length us, event | category | flops | bytes accessed | tf_op | source)
XLA Modules:
  0.0 111.6 jit_solution(5561320971519217682)
XLA Ops:
  0.6 0.9 collective-permute-start
  1.5 0.0 collective-permute-start.1
  1.6 0.5 collective-permute-start.2
  2.0 48.5 %attn.1 = (bf16[256,512,128]{2,1,0:T(8,128)(2,1)}, bf16[256,512,128]{2,1,0:T(8,128)(2,1)}, f32[256,1024]{1,0:T(8,128)}, bf16[256,1024]{1,0:T(8,128)(2,1)}, f32[32,256]{1,0:T(8,128)}) custom-call(s32[256]{0:T(256)} %lens_hbm.1, s32[8,256]{1,0:T(8,128)} %bitcast.19, bf16[1024]{0:T(1024)(128)(2,1)} %lnm_hbm.1, bf16[256,1024]{1,0:T(8,128)(2,1)} %h_hbm.1, ...), custom_call_target="tpu_custom_call" | custom-call | flops 40000000000 | bytes 140000000 | tf_op jit(solution)/shard_map/attn/pallas_call | solution.py:228
  50.6 0.0 collective-permute-done.wg_par
  50.6 0.0 collective-permute-done.1.wu_par
  50.6 0.0 collective-permute-done.2.wd_par
  50.6 59.1 %moe.1 = bf16[256,1024]{1,0:T(8,128)(2,1)} custom-call(bf16[256,1024]{1,0:T(8,128)(2,1)} %get-tuple-element.8.r_ref, f32[32,256]{1,0:T(8,128)} %get-tuple-element.9.gt_ref, f32[256,1024]{1,0:T(8,128)} %get-tuple-element.10.y_hbm, bf16[4,1024,512]{2,1,0:T(8,128)(2,1)} %wg_own.1, bf16[4,1024,512]{2,1,0:T(8,128)(2,1)} %wu_own.1, bf16[4,512,1024]{2,1,0:T(8,128)(2,1)} %wd_own.1, ...), custom_call_target="tpu_custom_call" | custom-call | flops 25999998976 | bytes 30000000 | tf_op jit(solution)/shard_map/moe/pallas_call | solution.py:388
  109.8 1.9 %copy.22 = bf16[256,1024]{1,0:T(8,128)(2,1)} copy(bf16[256,1024]{1,0:T(8,128)(2,1)} %moe.1) | data formatting | bytes 1048576
Async XLA Ops:
  0.6 49.9 %collective-permute-start = (bf16[4,1024,512]{2,1,0:T(8,128)(2,1)}, bf16[4,1024,512]{2,1,0:T(8,128)(2,1)}, u32[]{:S(2)}, u32[]{:S(2)}) collective-permute-start(bf16[4,1024,512]{2,1,0:T(8,128)(2,1)} %wg_own.1), channel_id=1, source_target_pairs={{0,1},{1,0},{2,3},{3,2},{4,5},{5,4},{6,7},{7,6}} | collective-permute-start | bytes 12582920 | tf_op jit(solution)/shard_map/ppermute | solution.py:411
  1.5 49.1 %collective-permute-start.1 = (bf16[4,1024,512]{2,1,0:T(8,128)(2,1)}, bf16[4,1024,512]{2,1,0:T(8,128)(2,1)}, u32[]{:S(2)}, u32[]{:S(2)}) collective-permute-start(bf16[4,1024,512]{2,1,0:T(8,128)(2,1)} %wu_own.1), channel_id=1, source_target_pairs={{0,1},{1,0},{2,3},{3,2},{4,5},{5,4},{6,7},{7,6}} | collective-permute-start | bytes 12582920 | tf_op jit(solution)/shard_map/ppermute | solution.py:412
  1.6 49.0 %collective-permute-start.2 = (bf16[4,512,1024]{2,1,0:T(8,128)(2,1)}, bf16[4,512,1024]{2,1,0:T(8,128)(2,1)}, u32[]{:S(2)}, u32[]{:S(2)}) collective-permute-start(bf16[4,512,1024]{2,1,0:T(8,128)(2,1)} %wd_own.1), channel_id=1, source_target_pairs={{0,1},{1,0},{2,3},{3,2},{4,5},{5,4},{6,7},{7,6}} | collective-permute-start | bytes 12582920 | tf_op jit(solution)/shard_map/ppermute | solution.py:413
where the time goes:
time: 112 us
  Pallas kernels  108 us (96%)
  local copies, waits for them, and re-layouts  1.87 us (2%)
  starting transfers between devices  1.39 us (1%)
    pallas_call x1, Pallas kernels, moe_call(): pl.pallas_call(moe_body, out_shape=jax.ShapeDtypeStruct((n, d), BF), in_s...  59.1 us
    pallas_call x1, Pallas kernels, attn_call(): pl.pallas_call(functools.partial(attn_body, cfg + (lo, n, first, last)),...  48.5 us
  transfers between devices with their start and end apart: 3, of which 0 were waited for; matrix products, arithmetic and copies ran while one was open for 0% of the time, Pallas kernels for 43%

commit v1 on v0

--- a/solution.py
+++ b/solution.py
@@ -188,7 +188,7 @@
     for j in range(nb):
         cout(steps - nb + j, 0).wait(); cout(steps - nb + j, 1).wait()
 
-def attn_call(hidden, kc, vc, seq_lens, expert_ids, ln_attn, w_q, w_k, w_v, q_gain, k_gain, w_o, ln_moe, w_router, lo, n, prev=None, cfg=(8, 8, 3)):
+def attn_call(hidden, kc, vc, seq_lens, expert_ids, ln_attn, w_q, w_k, w_v, q_gain, k_gain, w_o, ln_moe, w_router, lo, n, prev=None, cfg=(8, 8, 2)):
     ntot, d = hidden.shape
     _, dk, t = kc.shape
     hd = q_gain.shape[0]
@@ -236,8 +236,8 @@
     return c.transpose(0, 2, 3, 1).reshape(n, nk*hd, t), lambda z: z.reshape(n, nk, hd, t).transpose(0, 3, 1, 2)
 
 
-def moe_body(r_ref, gt_ref, y_hbm, wg_own, wu_own, wd_own, wg_par, wu_par, wd_par, out_ref,
-             wg, wu, wd, xr, gts, y_ref, act, acc, rbuf, wsem, ysem, agsem_s, agsem_r, gsem_s, gsem_r, rssem_s, rssem_r):
+def moe_body(r_hbm, gt_hbm, y_hbm, wg_own, wu_own, wd_own, wg_par, wu_par, wd_par, out_ref,
+             wg, wu, wd, r_ref, gt_ref, xr, gts, y_ref, act, acc, rbuf, wsem, ysem, agsem_s, agsem_r, gsem_s, gsem_r, rssem_s, rssem_r):
     me = lax.axis_index('ep')
     core = me % 2
     xpos = (me // 2) % 2
@@ -249,6 +249,9 @@
     hr, hc = acc.shape[3], acc.shape[4]
     ff = wg.shape[2]
 
+    mine = [pltpu.make_async_copy(a, b, ysem.at[i]) for i, (a, b) in enumerate(((r_hbm, r_ref), (gt_hbm, gt_ref)))]
+    for c in mine:
+        c.start()
     barrier = pltpu.get_barrier_semaphore()
     for p in peers[1:]:
         pl.semaphore_signal(barrier, inc=1, device_id={"ep": p}, device_id_type=pl.DeviceIdType.MESH)
@@ -263,8 +266,10 @@
     for e in range(1, ahead):
         for c in wcopy(jnp.int32(e), True):
             c.start()
-    ycopy = pltpu.make_async_copy(y_hbm, y_ref, ysem.at[0])
+    ycopy = pltpu.make_async_copy(y_hbm, y_ref, ysem.at[2])
     ycopy.start()
+    for c in mine:
+        c.wait()
     pl.semaphore_wait(barrier, 3)
 
     def remote(src, dst, ss, rs, p):
@@ -387,11 +392,11 @@
     dma = pltpu.SemaphoreType.DMA
     return pl.pallas_call(moe_body,
         out_shape=jax.ShapeDtypeStruct((n, d), BF),
-        in_specs=[vm, vm] + [an]*7, out_specs=vm,
+        in_specs=[an]*9, out_specs=vm,
         scratch_shapes=[pltpu.VMEM((2*nl, d, ff), BF), pltpu.VMEM((2*nl, d, ff), BF), pltpu.VMEM((2*nl, ff, d), BF),
-            pltpu.VMEM((3, n, d), BF), pltpu.VMEM((3, 2*nl, n), F32), pltpu.VMEM((n, d), F32), pltpu.VMEM((n, ff), BF),
+            pltpu.VMEM(r.shape, BF), pltpu.VMEM(gt.shape, F32), pltpu.VMEM((3, n, d), BF), pltpu.VMEM((3, 2*nl, n), F32), pltpu.VMEM((n, d), F32), pltpu.VMEM((n, ff), BF),
             pltpu.VMEM((4, 2, 2, n//2, d//2), F32), pltpu.VMEM((6, 2, n//2, d//2), F32),
-            dma((3, 2*nl)), dma((1,)), dma((3, 2)), dma((3, 2)), dma((3,)), dma((3,)), dma((6, 2)), dma((6, 2))],
+            dma((3, 2*nl)), dma((3,)), dma((3, 2)), dma((3, 2)), dma((3,)), dma((3,)), dma((6, 2)), dma((6, 2))],
         compiler_params=pltpu.CompilerParams(vmem_limit_bytes=67043328, collective_id=1, has_side_effects=True), name="moe",
         cost_estimate=pl.CostEstimate(flops=26*10**9, bytes_accessed=30*10**6, transcendentals=0),
     )(r, gt, y, w_gate, w_up, w_down, wg_p, wu_p, wd_p)

time: 112 us -> 111 us (level)
  transfers between devices with their start and end apart: 3 -> 3, of which waited for: 0 -> 0; matrix products, arithmetic and copies ran while one was open for 0% -> 0% of each run, Pallas kernels for 43% -> 44%
where the time goes in v1:
time: 111 us
  Pallas kernels  107 us (96%)
  local copies, waits for them, and re-layouts  1.87 us (2%)
  starting transfers between devices  1.39 us (1%)
    pallas_call x1, Pallas kernels, moe_call(): pl.pallas_call(moe_body, out_shape=jax.ShapeDtypeStruct((n, d), BF), in_s...  58.4 us
    pallas_call x1, Pallas kernels, attn_call(): pl.pallas_call(functools.partial(attn_body, cfg + (lo, n, first, last)),...  48.5 us
  transfers between devices with their start and end apart: 3, of which 0 were waited for; matrix products, arithmetic and copies ran while one was open for 0% of the time, Pallas kernels for 44%

profile of v1, /device:TPU:0, one launch (start us, length us, event | category | flops | bytes accessed | tf_op | source)
XLA Modules:
  0.0 110.8 jit_solution(2789887474773989712)
XLA Ops:
  0.6 0.9 collective-permute-start
  1.5 0.0 collective-permute-start.1
  1.6 0.5 collective-permute-start.2
  2.0 48.5 %attn.1 = (bf16[256,512,128]{2,1,0:T(8,128)(2,1)}, bf16[256,512,128]{2,1,0:T(8,128)(2,1)}, f32[256,1024]{1,0:T(8,128)}, bf16[256,1024]{1,0:T(8,128)(2,1)}, f32[32,256]{1,0:T(8,128)}) custom-call(s32[256]{0:T(256)} %lens_hbm.1, s32[8,256]{1,0:T(8,128)} %bitcast.19, bf16[1024]{0:T(1024)(128)(2,1)} %lnm_hbm.1, bf16[256,1024]{1,0:T(8,128)(2,1)} %h_hbm.1, ...), custom_call_target="tpu_custom_call" | custom-call | flops 40000000000 | bytes 140000000 | tf_op jit(solution)/shard_map/attn/pallas_call | solution.py:228
  50.5 0.0 collective-permute-done.wg_par
  50.5 0.0 collective-permute-done.1.wu_par
  50.5 0.0 collective-permute-done.2.wd_par
  50.6 58.4 %moe.1 = bf16[256,1024]{1,0:T(8,128)(2,1)} custom-call(bf16[256,1024]{1,0:T(8,128)(2,1)} %get-tuple-element.8.r_hbm, f32[32,256]{1,0:T(8,128)} %get-tuple-element.9.gt_hbm, f32[256,1024]{1,0:T(8,128)} %get-tuple-element.10.y_hbm, bf16[4,1024,512]{2,1,0:T(8,128)(2,1)} %wg_own.1, bf16[4,1024,512]{2,1,0:T(8,128)(2,1)} %wu_own.1, bf16[4,512,1024]{2,1,0:T(8,128)(2,1)} %wd_own.1, ...), custom_call_target="tpu_custom_call" | custom-call | flops 25999998976 | bytes 30000000 | tf_op jit(solution)/shard_map/moe/pallas_call | solution.py:393
  109.0 1.9 %copy.22 = bf16[256,1024]{1,0:T(8,128)(2,1)} copy(bf16[256,1024]{1,0:T(8,128)(2,1)} %moe.1) | data formatting | bytes 1048576
Async XLA Ops:
  0.6 49.9 %collective-permute-start = (bf16[4,1024,512]{2,1,0:T(8,128)(2,1)}, bf16[4,1024,512]{2,1,0:T(8,128)(2,1)}, u32[]{:S(2)}, u32[]{:S(2)}) collective-permute-start(bf16[4,1024,512]{2,1,0:T(8,128)(2,1)} %wg_own.1), channel_id=1, source_target_pairs={{0,1},{1,0},{2,3},{3,2},{4,5},{5,4},{6,7},{7,6}} | collective-permute-start | bytes 12582920 | tf_op jit(solution)/shard_map/ppermute | solution.py:416
  1.5 49.0 %collective-permute-start.1 = (bf16[4,1024,512]{2,1,0:T(8,128)(2,1)}, bf16[4,1024,512]{2,1,0:T(8,128)(2,1)}, u32[]{:S(2)}, u32[]{:S(2)}) collective-permute-start(bf16[4,1024,512]{2,1,0:T(8,128)(2,1)} %wu_own.1), channel_id=1, source_target_pairs={{0,1},{1,0},{2,3},{3,2},{4,5},{5,4},{6,7},{7,6}} | collective-permute-start | bytes 12582920 | tf_op jit(solution)/shard_map/ppermute | solution.py:417
  1.6 49.0 %collective-permute-start.2 = (bf16[4,512,1024]{2,1,0:T(8,128)(2,1)}, bf16[4,512,1024]{2,1,0:T(8,128)(2,1)}, u32[]{:S(2)}, u32[]{:S(2)}) collective-permute-start(bf16[4,512,1024]{2,1,0:T(8,128)(2,1)} %wd_own.1), channel_id=1, source_target_pairs={{0,1},{1,0},{2,3},{3,2},{4,5},{5,4},{6,7},{7,6}} | collective-permute-start | bytes 12582920 | tf_op jit(solution)/shard_map/ppermute | solution.py:418

commit v2 on v1

--- a/solution.py
+++ b/solution.py
@@ -267,7 +267,6 @@
         for c in wcopy(jnp.int32(e), True):
             c.start()
     ycopy = pltpu.make_async_copy(y_hbm, y_ref, ysem.at[2])
-    ycopy.start()
     for c in mine:
         c.wait()
     pl.semaphore_wait(barrier, 3)
@@ -288,6 +287,8 @@
     h0, h1 = pl.ds(0, hr), pl.ds(hr, hr)
     relay = [remote(xr.at[Y-1, h0], xr.at[D-1, h0], agsem_s.at[2, 0], agsem_r.at[2, 0], peers[X]),
              remote(xr.at[X-1, h1], xr.at[D-1, h1], agsem_s.at[2, 1], agsem_r.at[2, 1], peers[Y])]
+
+    ycopy.start()
 
     def gates(b):
         if b == OWN:
@@ -326,7 +327,7 @@
                 for i, (b, h) in enumerate(blocks):
                     acc[b, h, q//2, :, s:s+w] = acc[b, h, q//2, :, s:s+w] + f[i*hr:(i+1)*hr]
             return carry
-        lax.fori_loop(0, n_exp, step, 0, unroll=1 if first else 2)
+        lax.fori_loop(0, n_exp, step, 0, unroll=1 if first else 4)
 
     def rs(i, h, src, p):
         return remote(src, rbuf.at[i, h], rssem_s.at[i, h], rssem_r.at[i, h], p)

time: 111 us -> 110 us (level)
  no operation moved by 1% of the time
where the time goes in v2:
time: 110 us
  Pallas kernels  106 us (96%)
  local copies, waits for them, and re-layouts  1.87 us (2%)
  starting transfers between devices  1.39 us (1%)
    pallas_call x1, Pallas kernels, moe_call(): pl.pallas_call(moe_body, out_shape=jax.ShapeDtypeStruct((n, d), BF), in_s...  57.7 us
    pallas_call x1, Pallas kernels, attn_call(): pl.pallas_call(functools.partial(attn_body, cfg + (lo, n, first, last)),...  48.4 us
  transfers between devices with their start and end apart: 3, of which 0 were waited for; matrix products, arithmetic and copies ran while one was open for 0% of the time, Pallas kernels for 44%

profile of v2, /device:TPU:0, one launch (start us, length us, event | category | flops | bytes accessed | tf_op | source)
XLA Modules:
  0.0 110.1 jit_solution(2398615739422221439)
XLA Ops:
  0.6 0.9 collective-permute-start
  1.5 0.0 collective-permute-start.1
  1.6 0.5 collective-permute-start.2
  2.0 48.4 %attn.1 = (bf16[256,512,128]{2,1,0:T(8,128)(2,1)}, bf16[256,512,128]{2,1,0:T(8,128)(2,1)}, f32[256,1024]{1,0:T(8,128)}, bf16[256,1024]{1,0:T(8,128)(2,1)}, f32[32,256]{1,0:T(8,128)}) custom-call(s32[256]{0:T(256)} %lens_hbm.1, s32[8,256]{1,0:T(8,128)} %bitcast.19, bf16[1024]{0:T(1024)(128)(2,1)} %lnm_hbm.1, bf16[256,1024]{1,0:T(8,128)(2,1)} %h_hbm.1, ...), custom_call_target="tpu_custom_call" | custom-call | flops 40000000000 | bytes 140000000 | tf_op jit(solution)/shard_map/attn/pallas_call | solution.py:228
  50.5 0.0 collective-permute-done.wg_par
  50.5 0.0 collective-permute-done.1.wu_par
  50.5 0.0 collective-permute-done.2.wd_par
  50.5 57.7 %moe.1 = bf16[256,1024]{1,0:T(8,128)(2,1)} custom-call(bf16[256,1024]{1,0:T(8,128)(2,1)} %get-tuple-element.8.r_hbm, f32[32,256]{1,0:T(8,128)} %get-tuple-element.9.gt_hbm, f32[256,1024]{1,0:T(8,128)} %get-tuple-element.10.y_hbm, bf16[4,1024,512]{2,1,0:T(8,128)(2,1)} %wg_own.1, bf16[4,1024,512]{2,1,0:T(8,128)(2,1)} %wu_own.1, bf16[4,512,1024]{2,1,0:T(8,128)(2,1)} %wd_own.1, ...), custom_call_target="tpu_custom_call" | custom-call | flops 25999998976 | bytes 30000000 | tf_op jit(solution)/shard_map/moe/pallas_call | solution.py:394
  108.2 1.9 %copy.22 = bf16[256,1024]{1,0:T(8,128)(2,1)} copy(bf16[256,1024]{1,0:T(8,128)(2,1)} %moe.1) | data formatting | bytes 1048576
Async XLA Ops:
  0.6 49.8 %collective-permute-start = (bf16[4,1024,512]{2,1,0:T(8,128)(2,1)}, bf16[4,1024,512]{2,1,0:T(8,128)(2,1)}, u32[]{:S(2)}, u32[]{:S(2)}) collective-permute-start(bf16[4,1024,512]{2,1,0:T(8,128)(2,1)} %wg_own.1), channel_id=1, source_target_pairs={{0,1},{1,0},{2,3},{3,2},{4,5},{5,4},{6,7},{7,6}} | collective-permute-start | bytes 12582920 | tf_op jit(solution)/shard_map/ppermute | solution.py:417
  1.5 49.0 %collective-permute-start.1 = (bf16[4,1024,512]{2,1,0:T(8,128)(2,1)}, bf16[4,1024,512]{2,1,0:T(8,128)(2,1)}, u32[]{:S(2)}, u32[]{:S(2)}) collective-permute-start(bf16[4,1024,512]{2,1,0:T(8,128)(2,1)} %wu_own.1), channel_id=1, source_target_pairs={{0,1},{1,0},{2,3},{3,2},{4,5},{5,4},{6,7},{7,6}} | collective-permute-start | bytes 12582920 | tf_op jit(solution)/shard_map/ppermute | solution.py:418
  1.6 48.9 %collective-permute-start.2 = (bf16[4,512,1024]{2,1,0:T(8,128)(2,1)}, bf16[4,512,1024]{2,1,0:T(8,128)(2,1)}, u32[]{:S(2)}, u32[]{:S(2)}) collective-permute-start(bf16[4,512,1024]{2,1,0:T(8,128)(2,1)} %wd_own.1), channel_id=1, source_target_pairs={{0,1},{1,0},{2,3},{3,2},{4,5},{5,4},{6,7},{7,6}} | collective-permute-start | bytes 12582920 | tf_op jit(solution)/shard_map/ppermute | solution.py:419
